TPU v7x, 32 devices: a whole 2x2x4 slice. The times are simulated.
32 devices in a mesh: dp: 4 (over z), row: 2 (over y), col: 4 (over x, core).
Axes of the slice: x: 2, y: 2, z: 4, core: 2. Of those that a mesh axis runs over, the one named last changes fastest.
Arguments:
- activations: bfloat16 [4096, 4096], P('dp', 'col'), may hold values from -6 to 6
- out_grad: bfloat16 [4096, 14336], P('dp', 'row'), may hold values from -6 to 6
- weight: float32 [2, 7168, 4096], P('row', 'dp', 'col'), as said below
- step_size: float32 [2, 7168], P('row'), may hold values from 0.001 to 0.016
Outputs:
- input_grad: bfloat16 [4096, 4096], P(('dp', 'row'), 'col')
- weight_grad: float32 [2, 7168, 4096], P('row', 'dp', 'col')
- step_grad: float32 [2, 7168], P('row', 'dp')
Inputs may be any that keep to these rules, and one draw needn't show every extreme that they name: Each latent weight divided by its row's step lies at least 0.1 away from every multiple of one half.
All inputs are finite; a program needn't handle non-finite values.
Results may differ from a plain program's by a relative error of at most 0.0096.
Values may be sent and summed in bfloat16 or wider, within the bound.
A program may use at most 128 MiB of HBM per device.

v0:
```python
import jax
import jax.numpy as jnp
from jax import lax
from jax.sharding import PartitionSpec as P

D = 4096


def quantize(latent, scales):
    ratio = latent / scales[:, None]
    clipped = jnp.clip(ratio, -8.0, 7.0)
    levels = jnp.floor(clipped + 0.5)
    inside = jnp.where((ratio >= -8.0) & (ratio <= 7.0), 1.0, 0.0).astype(jnp.float32)
    factor = jnp.where(inside > 0.5, levels - ratio, clipped)
    quantized = (levels * scales[:, None]).astype(jnp.bfloat16)
    return (quantized, inside, factor)


def shift(block, axis, count, by):
    return lax.ppermute(block, axis, [(i, (i + by) % count) for i in range(count)])


def swap(block, axis, count, bit):
    return lax.ppermute(block, axis, [(i, i ^ bit) for i in range(count)])


def gather_rows(block, axis, count):
    position = lax.axis_index(axis)
    bit = 1
    bits = []
    while bit < count:
        bits.append(bit)
        bit *= 2
    pieces = {0: block}
    for bit in reversed(bits):
        held = dict(pieces)
        for key in held:
            pieces[key ^ bit] = swap(held[key], axis, count, bit)
    parts = [pieces[key] for key in range(count)]
    for bit in bits:
        flag = position & bit != 0
        parts = [jnp.where(flag, parts[key ^ bit], parts[key]) for key in range(count)]
    return jnp.concatenate(parts, axis=0)


def make_shards(n_dp, n_row, n_col):

    def shards(activations, out_grad, weight, step_size):
        own_count = weight.shape[1]
        tokens = out_grad.shape[0]
        dp = lax.axis_index("dp")
        row = lax.axis_index("row")
        col = lax.axis_index("col")
        scales = step_size[0]
        own_scales = lax.dynamic_slice_in_dim(scales, dp * own_count, own_count, 0)
        grad_factor = 1.0 / (7.0 * D) ** 0.5
        share = tokens // n_col
        half = tokens // n_row
        mine = lax.dynamic_slice_in_dim(out_grad, col * share, share, 0)
        ring = lax.dynamic_slice_in_dim(activations, row * half, half, 0)
        grads, acts = ([], [])
        for k in range(1, n_dp):
            target = (dp + k) % n_dp
            chunk = lax.dynamic_slice_in_dim(mine, target * own_count, own_count, 1)
            grads.append(shift(chunk, "dp", n_dp, k))
            ring = shift(ring, "dp", n_dp, 1)
            acts.append(ring)
        quantized, inside, factor = quantize(weight[0], own_scales)
        own_grad = lax.dynamic_slice_in_dim(out_grad, dp * own_count, own_count, 1)

        def reduced(grad):
            size = tokens
            bit = n_row // 2
            if bit == 0:
                return jnp.dot(grad, quantized, preferred_element_type=jnp.float32)
            size //= 2
            upper = (row // bit % 2).astype(jnp.int32)
            sent = lax.dynamic_slice_in_dim(grad, (1 - upper) * size, size, 0)
            kept = lax.dynamic_slice_in_dim(grad, upper * size, size, 0)
            out = jnp.dot(sent, quantized, preferred_element_type=jnp.float32).astype(jnp.bfloat16)
            came = swap(out, "row", n_row, bit)
            total = jnp.dot(kept, quantized, preferred_element_type=jnp.float32) + came.astype(
                jnp.float32
            )
            bit //= 2
            while bit:
                size //= 2
                upper = row // bit % 2 == 1
                low, high = (total[:size], total[size:])
                came = swap(jnp.where(upper, low, high).astype(jnp.bfloat16), "row", n_row, bit)
                total = jnp.where(upper, high, low) + came.astype(jnp.float32)
                bit //= 2
            return total

        products = lax.dot_general(
            own_grad, activations, (((0,), (0,)), ((), ())), preferred_element_type=jnp.float32
        )
        own_total = reduced(own_grad)
        running = None
        for k in range(1, n_dp):
            grad = gather_rows(grads[k - 1], "col", n_col)
            total = reduced(grad)
            if running is not None:
                total = total + running.astype(jnp.float32)
            running = shift(total.astype(jnp.bfloat16), "dp", n_dp, 1)
            act = gather_rows(acts[k - 1], "row", n_row)
            products = products + lax.dot_general(
                grad, act, (((0,), (0,)), ((), ())), preferred_element_type=jnp.float32
            )
        if running is not None:
            own_total = own_total + running.astype(jnp.float32)
        input_grad = own_total.astype(jnp.bfloat16)
        step_rows = lax.psum(jnp.sum(products * factor, axis=1) * grad_factor, "col")
        weight_grad = (products * inside)[None]
        return (input_grad, weight_grad, step_rows[None])

    return shards


def solution(mesh):
    in_specs = (P("dp", "col"), P("dp", "row"), P("row", "dp", "col"), P("row", None))
    out_specs = (P(("dp", "row"), "col"), P("row", "dp", "col"), P("row", "dp"))
    shards = make_shards(mesh.shape["dp"], mesh.shape["row"], mesh.shape["col"])
    return jax.shard_map(shards, mesh=mesh, in_specs=in_specs, out_specs=out_specs, check_vma=False)
```

profile of v0, /device:TPU:0, one launch (start us, length us, event | category | flops | bytes accessed | tf_op | source)
XLA Modules:
  0.0 330.7 jit_solution(6011322174611351139)
XLA Ops:
  6.3 4.7 %fusion.58 = (bf16[256,1792]{1,0:T(8,128)(2,1)}, bf16[256,1792]{1,0:T(8,128)(2,1)}, bf16[256,1792]{1,0:T(8,128)(2,1)S(1)}) fusion(bf16[1024,7168]{1,0:T(8,128)(2,1)} %param.5, s32[]{:T(128)S(6)} %select_n.223, s32[]{:T(128)S(6)} %select_n.226, s32[]{:T(128)S(6)} %select_n.237, s32[]{:T(128)S(6)} %select_n.248), kind=kLoop, calls=%fused_computation.92 | loop fusion | bytes 5505040 | tf_op jit(solution)/shard_map/dynamic_slice | solution.py:64
  12.6 20.0 %collective-permute-done.19 = bf16[512,1024]{1,0:T(8,128)(2,1)S(1)} collective-permute-done((bf16[512,1024]{1,0:T(8,128)(2,1)}, bf16[512,1024]{1,0:T(8,128)(2,1)S(1)}, u32[]{:S(2)}, u32[]{:S(2)}) %collective-permute-start.19) | collective-permute-done | bytes 1048608 | tf_op jit(solution)/shard_map/ppermute | solution.py:20
  36.1 16.3 %collective-permute-done.11 = bf16[256,1792]{1,0:T(8,128)(2,1)} collective-permute-done((bf16[256,1792]{1,0:T(8,128)(2,1)S(1)}, bf16[256,1792]{1,0:T(8,128)(2,1)}, u32[]{:S(2)}, u32[]{:S(2)}) %collective-permute-start.11) | collective-permute-done | bytes 917536 | tf_op jit(solution)/shard_map/ppermute | solution.py:20
  54.1 8.4 %copy.7 = f32[1,1792,1024]{1,2,0:T(8,128)} copy(f32[1,1792,1024]{2,1,0:T(8,128)} %param.6) | data formatting | bytes 14680064 | tf_op args[2]
  63.3 7.9 %collective-permute-done.1 = bf16[256,1792]{1,0:T(8,128)(2,1)} collective-permute-done((bf16[256,1792]{1,0:T(8,128)(2,1)}, bf16[256,1792]{1,0:T(8,128)(2,1)}, u32[]{:S(2)}, u32[]{:S(2)}) %collective-permute-start.1) | collective-permute-done | bytes 917536 | tf_op jit(solution)/shard_map/ppermute | solution.py:20
  72.7 37.7 %collective-permute-done.6 = bf16[256,1792]{1,0:T(8,128)(2,1)} collective-permute-done((bf16[256,1792]{1,0:T(8,128)(2,1)}, bf16[256,1792]{1,0:T(8,128)(2,1)}, u32[]{:S(2)}, u32[]{:S(2)}) %collective-permute-start.6) | collective-permute-done | bytes 917536 | tf_op jit(solution)/shard_map/ppermute | solution.py:20
  112.0 8.2 %fusion.1 = f32[1792,1024]{0,1:T(8,128)} fusion(bf16[1024,1024]{1,0:T(8,128)(2,1)S(1)} %copy-done, bf16[1024,7168]{1,0:T(8,128)(2,1)} %param.5, s32[]{:T(128)S(6)} %select_n.216), kind=kOutput, calls=%fused_computation.12 | convolution fusion | flops 3758096384 | bytes 13107204 | tf_op jit(solution)/shard_map/dot_general | solution.py:95
  122.3 10.7 %collective-permute-done.7 = bf16[256,1792]{1,0:T(8,128)(2,1)S(1)} collective-permute-done((bf16[256,1792]{1,0:T(8,128)(2,1)}, bf16[256,1792]{1,0:T(8,128)(2,1)S(1)}, u32[]{:S(2)}, u32[]{:S(2)}) %collective-permute-start.7) | collective-permute-done | bytes 917536 | tf_op jit(solution)/shard_map/ppermute | solution.py:24
  132.9 5.6 %collective-permute-done.21 = bf16[512,1024]{1,0:T(8,128)(2,1)S(1)} collective-permute-done((bf16[512,1024]{1,0:T(8,128)(2,1)S(1)}, bf16[512,1024]{1,0:T(8,128)(2,1)S(1)}, u32[]{:S(2)}, u32[]{:S(2)}) %collective-permute-start.21) | collective-permute-done | bytes 1048608 | tf_op jit(solution)/shard_map/ppermute | solution.py:20
  141.9 6.7 %fusion.3 = f32[1792,1024]{0,1:T(8,128)} fusion(bf16[512,1024]{1,0:T(8,128)(2,1)S(1)} %get-tuple-element.27, bf16[512,1024]{1,0:T(8,128)(2,1)S(1)} %get-tuple-element.26, bf16[256,1792]{1,0:T(8,128)(2,1)S(1)} %get-tuple-element.23, bf16[256,1792]{1,0:T(8,128)(2,1)S(1)} %get-tuple-element.22, bf16[256,1792]{1,0:T(8,128)(2,1)S(1)} %get-tuple-element.21, ...), kind=kOutput, calls=%fused_computation.14 | convolution fusion | flops 3776970752 | bytes 13107200 | tf_op jit(solution)/shard_map/dot_general | solution.py:107
  148.6 6.0 %collective-permute-start.23 = (bf16[512,1024]{1,0:T(8,128)(2,1)S(1)}, bf16[512,1024]{1,0:T(8,128)(2,1)S(1)}, u32[]{:S(2)}, u32[]{:S(2)}) collective-permute-start(bf16[512,1024]{1,0:T(8,128)(2,1)S(1)} %collective-permute-done.21), channel_id=1, source_target_pairs={{0,8},{8,16},{16,24},{24,0},{1,9},{9,17},{17,25},{25,1},{2,10},{10... | collective-permute-start | bytes 3145736 | tf_op jit(solution)/shard_map/ppermute | solution.py:20
  154.6 3.3 broadcast_select_fusion.29
  159.4 17.6 %collective-permute-done.23 = bf16[512,1024]{1,0:T(8,128)(2,1)S(1)} collective-permute-done((bf16[512,1024]{1,0:T(8,128)(2,1)S(1)}, bf16[512,1024]{1,0:T(8,128)(2,1)S(1)}, u32[]{:S(2)}, u32[]{:S(2)}) %collective-permute-start.23) | collective-permute-done | bytes 1048608 | tf_op jit(solution)/shard_map/ppermute | solution.py:20
  179.7 6.7 %fusion.7 = f32[1792,1024]{0,1:T(8,128)} fusion(bf16[512,1024]{1,0:T(8,128)(2,1)S(1)} %get-tuple-element.29, bf16[512,1024]{1,0:T(8,128)(2,1)S(1)} %get-tuple-element.28, bf16[256,1792]{1,0:T(8,128)(2,1)S(1)} %get-tuple-element.19, bf16[256,1792]{1,0:T(8,128)(2,1)S(1)} %get-tuple-element.18, bf16[256,1792]{1,0:T(8,128)(2,1)S(1)} %get-tuple-element.17, ...), kind=kOutput, calls=%fused_computation.18 | convolution fusion | flops 3776970752 | bytes 13107200 | tf_op jit(solution)/shard_map/dot_general | solution.py:107
  186.4 14.6 %collective-permute-done.24 = bf16[512,1024]{1,0:T(8,128)(2,1)S(1)} collective-permute-done((bf16[512,1024]{1,0:T(8,128)(2,1)S(1)}, bf16[512,1024]{1,0:T(8,128)(2,1)S(1)}, u32[]{:S(2)}, u32[]{:S(2)}) %collective-permute-start.24) | collective-permute-done | bytes 1048608 | tf_op jit(solution)/shard_map/ppermute | solution.py:24
  202.4 13.7 %add_add_fusion = f32[1792,1024]{0,1:T(8,128)} fusion(f32[1792,1024]{0,1:T(8,128)} %fusion.7, f32[1792,1024]{0,1:T(8,128)} %fusion.1, f32[1792,1024]{0,1:T(8,128)} %fusion.3, bf16[512,1024]{1,0:T(8,128)(2,1)} %get-tuple-element.25, bf16[512,1024]{1,0:T(8,128)(2,1)} %get-tuple-element.24, bf16[256,1792]{1,0:T(8,128)(2,1)} %get-tuple-element.15, ...), kind=kOutput, calls=%fused_computation.5 | convolution fusion | flops 3782475776 | bytes 35127296 | tf_op jit(solution)/shard_map/dot_general | solution.py:107
  216.2 8.0 %multiply_reduce_fusion = (f32[1792]{0:T(1024)S(1)}, f32[1,1792,1024]{1,2,0:T(8,128)}, bf16[1792,1024]{0,1:T(8,128)(2,1)S(1)}) fusion(f32[1792,1024]{0,1:T(8,128)} %add_add_fusion, f32[1792]{0:T(1024)S(1)} %dynamic-slice_reduce_fusion, f32[1,1792,1024]{1,2,0:T(8,128)S(1)} %bitcast.20), kind=kLoop, calls=%fused_computation.4 | loop fusion | flops 29358336 | bytes 25704448 | tf_op jit(solution)/shard_map/reduce_sum | solution.py:113
  224.2 3.1 fusion.39
  227.7 5.1 %pad_maximum_fusion.1 = bf16[1024,1792]{1,0:T(8,128)(2,1)S(1)} fusion(bf16[256,1792]{1,0:T(8,128)(2,1)} %copy-done.14, bf16[256,1792]{1,0:T(8,128)(2,1)} %copy-done.13, bf16[256,1792]{1,0:T(8,128)(2,1)S(1)} %copy-done.12, bf16[256,1792]{1,0:T(8,128)(2,1)S(1)} %copy-done.10), kind=kLoop, calls=%fused_computation.10 | loop fusion | flops 14680064 | bytes 7340032 | tf_op jit(solution)/shard_map/concatenate | solution.py:43
  236.6 17.0 %collective-permute-done.15 = bf16[512,1024]{1,0:T(8,128)(2,1)} collective-permute-done((bf16[512,1024]{1,0:T(8,128)(2,1)}, bf16[512,1024]{1,0:T(8,128)(2,1)}, u32[]{:S(2)}, u32[]{:S(2)}) %collective-permute-start.15) | collective-permute-done | bytes 1048608 | tf_op jit(solution)/shard_map/ppermute | solution.py:24
  253.6 3.3 %add_convert_fusion.3 = bf16[512,1024]{1,0:T(8,128)(2,1)S(1)} fusion(bf16[512,1024]{1,0:T(8,128)(2,1)} %collective-permute-done.15, bf16[1792,1024]{0,1:T(8,128)(2,1)S(1)} %copy-done.16, bf16[1024,1792]{1,0:T(8,128)(2,1)S(1)} %copy-done.3, s32[]{:T(128)S(6)} %select_n.214), kind=kOutput, calls=%fused_computation.28 | convolution fusion | flops 1880621056 | bytes 7602180 | tf_op jit(solution)/shard_map/dot_general | solution.py:82
  259.9 3.1 fusion.33
  263.6 12.4 %collective-permute-done.10 = bf16[512,1024]{1,0:T(8,128)(2,1)S(1)} collective-permute-done((bf16[512,1024]{1,0:T(8,128)(2,1)S(1)}, bf16[512,1024]{1,0:T(8,128)(2,1)S(1)}, u32[]{:S(2)}, u32[]{:S(2)}) %collective-permute-start.10) | collective-permute-done | bytes 1048608 | tf_op jit(solution)/shard_map/ppermute | solution.py:24
  275.9 3.7 %collective-permute-done.16 = bf16[512,1024]{1,0:T(8,128)(2,1)S(1)} collective-permute-done((bf16[512,1024]{1,0:T(8,128)(2,1)S(1)}, bf16[512,1024]{1,0:T(8,128)(2,1)S(1)}, u32[]{:S(2)}, u32[]{:S(2)}) %collective-permute-start.16) | collective-permute-done | bytes 1048608 | tf_op jit(solution)/shard_map/ppermute | solution.py:20
  279.7 3.1 add_convert_fusion.2
  282.8 5.9 %fusion.30 = bf16[512,1024]{1,0:T(8,128)(2,1)} fusion(bf16[1792,1024]{0,1:T(8,128)(2,1)} %copy-done.15, bf16[1024,7168]{1,0:T(8,128)(2,1)} %param.5, s32[]{:T(128)S(6)} %select_n.219, s32[]{:T(128)S(6)} %select_n.217), kind=kOutput, calls=%fused_computation.45 | convolution fusion | flops 1879572480 | bytes 6553608 | tf_op jit(solution)/shard_map/dot_general | solution.py:80
  289.2 9.2 %collective-permute-done.5 = bf16[512,1024]{1,0:T(8,128)(2,1)S(1)} collective-permute-done((bf16[512,1024]{1,0:T(8,128)(2,1)}, bf16[512,1024]{1,0:T(8,128)(2,1)S(1)}, u32[]{:S(2)}, u32[]{:S(2)}) %collective-permute-start.5) | collective-permute-done | bytes 1048608 | tf_op jit(solution)/shard_map/ppermute | solution.py:24
  298.4 5.7 %collective-permute-done.17 = bf16[512,1024]{1,0:T(8,128)(2,1)S(1)} collective-permute-done((bf16[512,1024]{1,0:T(8,128)(2,1)}, bf16[512,1024]{1,0:T(8,128)(2,1)S(1)}, u32[]{:S(2)}, u32[]{:S(2)}) %collective-permute-start.17) | collective-permute-done | bytes 1048608 | tf_op jit(solution)/shard_map/ppermute | solution.py:20
  304.2 3.1 add_convert_fusion.1
  307.3 8.4 %copy.8 = f32[1,1792,1024]{2,1,0:T(8,128)} copy(f32[1,1792,1024]{1,2,0:T(8,128)} %get-tuple-element.7) | data formatting | bytes 14680064
  315.7 6.7 %psum.7 = f32[1,1792]{1,0:T(1,128)} all-reduce(f32[1,1792]{1,0:T(1,128)S(1)} %broadcast_in_dim.19), channel_id=1, replica_groups=mesh['dp'=4,'row'=2,'col'=4] {'col'}, use_global_device_ids=true, to_apply=%region_1.2 | all-reduce | flops 1792 | bytes 14336 | tf_op jit(solution)/shard_map/psum | solution.py:113
  322.4 4.9 %fusion.28 = f32[512,1024]{1,0:T(8,128)S(1)} fusion(bf16[1792,1024]{0,1:T(8,128)(2,1)} %copy-done.15, bf16[1024,7168]{1,0:T(8,128)(2,1)} %param.5, s32[]{:T(128)S(6)} %select_n.215, s32[]{:T(128)S(6)} %select_n.217), kind=kOutput, calls=%fused_computation.43 | convolution fusion | flops 1879048192 | bytes 7602184 | tf_op jit(solution)/shard_map/dot_general | solution.py:82
  (90 shorter events, 39.0 us)
Async XLA Ops:
  3.3 29.3 %collective-permute-start.19 = (bf16[512,1024]{1,0:T(8,128)(2,1)}, bf16[512,1024]{1,0:T(8,128)(2,1)S(1)}, u32[]{:S(2)}, u32[]{:S(2)}) collective-permute-start(bf16[512,1024]{1,0:T(8,128)(2,1)} %constant_dynamic-slice_fusion), channel_id=1, source_target_pairs={{0,8},{8,16},{16,24},{24,0},{1,9},{9,17},{17,25},{25,1},{2,10},{10... | collective-permute-start | bytes 3145736 | tf_op jit(solution)/shard_map/ppermute | solution.py:20
  11.0 41.4 %collective-permute-start.11 = (bf16[256,1792]{1,0:T(8,128)(2,1)S(1)}, bf16[256,1792]{1,0:T(8,128)(2,1)}, u32[]{:S(2)}, u32[]{:S(2)}) collective-permute-start(bf16[256,1792]{1,0:T(8,128)(2,1)S(1)} %get-tuple-element.10), channel_id=1, source_target_pairs={{0,8},{8,16},{16,24},{24,0},{1,9},{9,17},{17,25},{25,1},{2,10},{10... | collective-permute-start | bytes 2752520 | tf_op jit(solution)/shard_map/ppermute | solution.py:20
  32.6 79.4 %collective-permute-start.20 = (bf16[512,1024]{1,0:T(8,128)(2,1)S(1)}, bf16[512,1024]{1,0:T(8,128)(2,1)}, u32[]{:S(2)}, u32[]{:S(2)}) collective-permute-start(bf16[512,1024]{1,0:T(8,128)(2,1)S(1)} %collective-permute-done.19), channel_id=1, source_target_pairs={{0,4},{4,0},{1,5},{5,1},{2,6},{6,2},{3,7},{7,3},{8,12},{12,8},{9,1... | collective-permute-start | bytes 3145736 | tf_op jit(solution)/shard_map/ppermute | solution.py:24
  34.3 36.9 %collective-permute-start.1 = (bf16[256,1792]{1,0:T(8,128)(2,1)}, bf16[256,1792]{1,0:T(8,128)(2,1)}, u32[]{:S(2)}, u32[]{:S(2)}) collective-permute-start(bf16[256,1792]{1,0:T(8,128)(2,1)} %get-tuple-element.8), channel_id=1, source_target_pairs={{0,24},{8,0},{16,8},{24,16},{1,25},{9,1},{17,9},{25,17},{2,26},{10... | collective-permute-start | bytes 2752520 | tf_op jit(solution)/shard_map/ppermute | solution.py:20
  36.1 74.4 %collective-permute-start.6 = (bf16[256,1792]{1,0:T(8,128)(2,1)}, bf16[256,1792]{1,0:T(8,128)(2,1)}, u32[]{:S(2)}, u32[]{:S(2)}) collective-permute-start(bf16[256,1792]{1,0:T(8,128)(2,1)} %get-tuple-element.9), channel_id=1, source_target_pairs={{0,16},{8,24},{16,0},{24,8},{1,17},{9,25},{17,1},{25,9},{2,18},{10... | collective-permute-start | bytes 2752520 | tf_op jit(solution)/shard_map/ppermute | solution.py:20
  52.4 59.6 %collective-permute-start.12 = (bf16[256,1792]{1,0:T(8,128)(2,1)}, bf16[256,1792]{1,0:T(8,128)(2,1)}, u32[]{:S(2)}, u32[]{:S(2)}) collective-permute-start(bf16[256,1792]{1,0:T(8,128)(2,1)} %collective-permute-done.11), channel_id=1, source_target_pairs={{0,2},{1,3},{2,0},{3,1},{4,6},{5,7},{6,4},{7,5},{8,10},{9,11},{10,... | collective-permute-start | bytes 2752520 | tf_op jit(solution)/shard_map/ppermute | solution.py:24
  63.3 58.9 %collective-permute-start.14 = (bf16[256,1792]{1,0:T(8,128)(2,1)}, bf16[256,1792]{1,0:T(8,128)(2,1)S(1)}, u32[]{:S(2)}, u32[]{:S(2)}) collective-permute-start(bf16[256,1792]{1,0:T(8,128)(2,1)} %collective-permute-done.11), channel_id=1, source_target_pairs={{0,1},{1,0},{2,3},{3,2},{4,5},{5,4},{6,7},{7,6},{8,9},{9,8},{10,11... | collective-permute-start | bytes 2752520 | tf_op jit(solution)/shard_map/ppermute | solution.py:24
  71.2 50.4 %collective-permute-start.2 = (bf16[256,1792]{1,0:T(8,128)(2,1)}, bf16[256,1792]{1,0:T(8,128)(2,1)S(1)}, u32[]{:S(2)}, u32[]{:S(2)}) collective-permute-start(bf16[256,1792]{1,0:T(8,128)(2,1)} %collective-permute-done.1), channel_id=1, source_target_pairs={{0,2},{1,3},{2,0},{3,1},{4,6},{5,7},{6,4},{7,5},{8,10},{9,11},{10,... | collective-permute-start | bytes 2752520 | tf_op jit(solution)/shard_map/ppermute | solution.py:24
  110.5 22.4 %collective-permute-start.7 = (bf16[256,1792]{1,0:T(8,128)(2,1)}, bf16[256,1792]{1,0:T(8,128)(2,1)S(1)}, u32[]{:S(2)}, u32[]{:S(2)}) collective-permute-start(bf16[256,1792]{1,0:T(8,128)(2,1)} %collective-permute-done.6), channel_id=1, source_target_pairs={{0,2},{1,3},{2,0},{3,1},{4,6},{5,7},{6,4},{7,5},{8,10},{9,11},{10,... | collective-permute-start | bytes 2752520 | tf_op jit(solution)/shard_map/ppermute | solution.py:24
  112.0 26.6 %collective-permute-start.21 = (bf16[512,1024]{1,0:T(8,128)(2,1)S(1)}, bf16[512,1024]{1,0:T(8,128)(2,1)S(1)}, u32[]{:S(2)}, u32[]{:S(2)}) collective-permute-start(bf16[512,1024]{1,0:T(8,128)(2,1)S(1)} %collective-permute-done.19), channel_id=1, source_target_pairs={{0,8},{8,16},{16,24},{24,0},{1,9},{9,17},{17,25},{25,1},{2,10},{10... | collective-permute-start | bytes 3145736 | tf_op jit(solution)/shard_map/ppermute | solution.py:20
  112.0 26.6 %collective-permute-start.13 = (bf16[256,1792]{1,0:T(8,128)(2,1)}, bf16[256,1792]{1,0:T(8,128)(2,1)S(1)}, u32[]{:S(2)}, u32[]{:S(2)}) collective-permute-start(bf16[256,1792]{1,0:T(8,128)(2,1)} %collective-permute-done.12), channel_id=1, source_target_pairs={{0,1},{1,0},{2,3},{3,2},{4,5},{5,4},{6,7},{7,6},{8,9},{9,8},{10,11... | collective-permute-start | bytes 2752520 | tf_op jit(solution)/shard_map/ppermute | solution.py:24
  121.6 27.0 %collective-permute-start.4 = (bf16[256,1792]{1,0:T(8,128)(2,1)}, bf16[256,1792]{1,0:T(8,128)(2,1)S(1)}, u32[]{:S(2)}, u32[]{:S(2)}) collective-permute-start(bf16[256,1792]{1,0:T(8,128)(2,1)} %collective-permute-done.1), channel_id=1, source_target_pairs={{0,1},{1,0},{2,3},{3,2},{4,5},{5,4},{6,7},{7,6},{8,9},{9,8},{10,11... | collective-permute-start | bytes 2752520 | tf_op jit(solution)/shard_map/ppermute | solution.py:24
  122.2 35.7 %collective-permute-start.9 = (bf16[256,1792]{1,0:T(8,128)(2,1)}, bf16[256,1792]{1,0:T(8,128)(2,1)S(1)}, u32[]{:S(2)}, u32[]{:S(2)}) collective-permute-start(bf16[256,1792]{1,0:T(8,128)(2,1)} %collective-permute-done.6), channel_id=1, source_target_pairs={{0,1},{1,0},{2,3},{3,2},{4,5},{5,4},{6,7},{7,6},{8,9},{9,8},{10,11... | collective-permute-start | bytes 2752520 | tf_op jit(solution)/shard_map/ppermute | solution.py:24
  132.9 21.7 %collective-permute-start.3 = (bf16[256,1792]{1,0:T(8,128)(2,1)S(1)}, bf16[256,1792]{1,0:T(8,128)(2,1)S(1)}, u32[]{:S(2)}, u32[]{:S(2)}) collective-permute-start(bf16[256,1792]{1,0:T(8,128)(2,1)S(1)} %collective-permute-done.2), channel_id=1, source_target_pairs={{0,1},{1,0},{2,3},{3,2},{4,5},{5,4},{6,7},{7,6},{8,9},{9,8},{10,11... | collective-permute-start | bytes 2752520 | tf_op jit(solution)/shard_map/ppermute | solution.py:24
  138.5 19.4 %collective-permute-start.8 = (bf16[256,1792]{1,0:T(8,128)(2,1)S(1)}, bf16[256,1792]{1,0:T(8,128)(2,1)S(1)}, u32[]{:S(2)}, u32[]{:S(2)}) collective-permute-start(bf16[256,1792]{1,0:T(8,128)(2,1)S(1)} %collective-permute-done.7), channel_id=1, source_target_pairs={{0,1},{1,0},{2,3},{3,2},{4,5},{5,4},{6,7},{7,6},{8,9},{9,8},{10,11... | collective-permute-start | bytes 2752520 | tf_op jit(solution)/shard_map/ppermute | solution.py:24
  138.5 41.0 %collective-permute-start.22 = (bf16[512,1024]{1,0:T(8,128)(2,1)S(1)}, bf16[512,1024]{1,0:T(8,128)(2,1)S(1)}, u32[]{:S(2)}, u32[]{:S(2)}) collective-permute-start(bf16[512,1024]{1,0:T(8,128)(2,1)S(1)} %collective-permute-done.21), channel_id=1, source_target_pairs={{0,4},{4,0},{1,5},{5,1},{2,6},{6,2},{3,7},{7,3},{8,12},{12,8},{9,1... | collective-permute-start | bytes 3145736 | tf_op jit(solution)/shard_map/ppermute | solution.py:24
  148.6 28.3 %collective-permute-start.23 = (bf16[512,1024]{1,0:T(8,128)(2,1)S(1)}, bf16[512,1024]{1,0:T(8,128)(2,1)S(1)}, u32[]{:S(2)}, u32[]{:S(2)}) collective-permute-start(bf16[512,1024]{1,0:T(8,128)(2,1)S(1)} %collective-permute-done.21), channel_id=1, source_target_pairs={{0,8},{8,16},{16,24},{24,0},{1,9},{9,17},{17,25},{25,1},{2,10},{10... | collective-permute-start | bytes 3145736 | tf_op jit(solution)/shard_map/ppermute | solution.py:20
  159.4 20.3 %copy-start.9 = (bf16[256,1792]{1,0:T(8,128)(2,1)}, bf16[256,1792]{1,0:T(8,128)(2,1)S(1)}, u32[]{:S(2)}) copy-start(bf16[256,1792]{1,0:T(8,128)(2,1)S(1)} %get-tuple-element.16) | copy-start | bytes 2752516
  177.0 24.0 %collective-permute-start.24 = (bf16[512,1024]{1,0:T(8,128)(2,1)S(1)}, bf16[512,1024]{1,0:T(8,128)(2,1)S(1)}, u32[]{:S(2)}, u32[]{:S(2)}) collective-permute-start(bf16[512,1024]{1,0:T(8,128)(2,1)S(1)} %collective-permute-done.23), channel_id=1, source_target_pairs={{0,4},{4,0},{1,5},{5,1},{2,6},{6,2},{3,7},{7,3},{8,12},{12,8},{9,1... | collective-permute-start | bytes 3145736 | tf_op jit(solution)/shard_map/ppermute | solution.py:24
  227.2 26.4 %collective-permute-start.15 = (bf16[512,1024]{1,0:T(8,128)(2,1)}, bf16[512,1024]{1,0:T(8,128)(2,1)}, u32[]{:S(2)}, u32[]{:S(2)}) collective-permute-start(bf16[512,1024]{1,0:T(8,128)(2,1)} %fusion.39), channel_id=1, source_target_pairs={{0,4},{4,0},{1,5},{5,1},{2,6},{6,2},{3,7},{7,3},{8,12},{12,8},{9,1... | collective-permute-start | bytes 3145736 | tf_op jit(solution)/shard_map/ppermute | solution.py:24
  232.9 20.7 %copy-start.3 = (bf16[1024,1792]{1,0:T(8,128)(2,1)S(1)}, bf16[1024,1792]{1,0:T(8,128)(2,1)}, u32[]{:S(2)}) copy-start(bf16[1024,1792]{1,0:T(8,128)(2,1)} %pad_maximum_fusion.2) | copy-start | bytes 11010052
  235.0 24.6 %copy-start.6 = (bf16[256,1792]{1,0:T(8,128)(2,1)S(1)}, bf16[256,1792]{1,0:T(8,128)(2,1)}, u32[]{:S(2)}) copy-start(bf16[256,1792]{1,0:T(8,128)(2,1)} %get-tuple-element.13) | copy-start | bytes 2752516
  235.0 24.5 %copy-start.7 = (bf16[256,1792]{1,0:T(8,128)(2,1)S(1)}, bf16[256,1792]{1,0:T(8,128)(2,1)}, u32[]{:S(2)}) copy-start(bf16[256,1792]{1,0:T(8,128)(2,1)} %get-tuple-element.14) | copy-start | bytes 2752516
  235.0 24.5 %copy-start.8 = (bf16[256,1792]{1,0:T(8,128)(2,1)S(1)}, bf16[256,1792]{1,0:T(8,128)(2,1)}, u32[]{:S(2)}) copy-start(bf16[256,1792]{1,0:T(8,128)(2,1)} %get-tuple-element.15) | copy-start | bytes 2752516
  235.0 40.9 %collective-permute-start.10 = (bf16[512,1024]{1,0:T(8,128)(2,1)S(1)}, bf16[512,1024]{1,0:T(8,128)(2,1)S(1)}, u32[]{:S(2)}, u32[]{:S(2)}) collective-permute-start(bf16[512,1024]{1,0:T(8,128)(2,1)S(1)} %fusion.36), channel_id=1, source_target_pairs={{0,4},{4,0},{1,5},{5,1},{2,6},{6,2},{3,7},{7,3},{8,12},{12,8},{9,1... | collective-permute-start | bytes 3145736 | tf_op jit(solution)/shard_map/ppermute | solution.py:24
  256.9 22.8 %collective-permute-start.16 = (bf16[512,1024]{1,0:T(8,128)(2,1)S(1)}, bf16[512,1024]{1,0:T(8,128)(2,1)S(1)}, u32[]{:S(2)}, u32[]{:S(2)}) collective-permute-start(bf16[512,1024]{1,0:T(8,128)(2,1)S(1)} %add_convert_fusion.3), channel_id=1, source_target_pairs={{0,8},{8,16},{16,24},{24,0},{1,9},{9,17},{17,25},{25,1},{2,10},{10... | collective-permute-start | bytes 3145736 | tf_op jit(solution)/shard_map/ppermute | solution.py:20
  263.1 35.4 %collective-permute-start.5 = (bf16[512,1024]{1,0:T(8,128)(2,1)}, bf16[512,1024]{1,0:T(8,128)(2,1)S(1)}, u32[]{:S(2)}, u32[]{:S(2)}) collective-permute-start(bf16[512,1024]{1,0:T(8,128)(2,1)} %fusion.33), channel_id=1, source_target_pairs={{0,4},{4,0},{1,5},{5,1},{2,6},{6,2},{3,7},{7,3},{8,12},{12,8},{9,1... | collective-permute-start | bytes 3145736 | tf_op jit(solution)/shard_map/ppermute | solution.py:24
  282.8 21.4 %collective-permute-start.17 = (bf16[512,1024]{1,0:T(8,128)(2,1)}, bf16[512,1024]{1,0:T(8,128)(2,1)S(1)}, u32[]{:S(2)}, u32[]{:S(2)}) collective-permute-start(bf16[512,1024]{1,0:T(8,128)(2,1)} %add_convert_fusion.2), channel_id=1, source_target_pairs={{0,8},{8,16},{16,24},{24,0},{1,9},{9,17},{17,25},{25,1},{2,10},{10... | collective-permute-start | bytes 3145736 | tf_op jit(solution)/shard_map/ppermute | solution.py:20
  282.8 21.4 %copy-start.5 = (bf16[1024,1792]{1,0:T(8,128)(2,1)S(1)}, bf16[1024,1792]{1,0:T(8,128)(2,1)}, u32[]{:S(2)}) copy-start(bf16[1024,1792]{1,0:T(8,128)(2,1)} %copy-done.4) | copy-start | bytes 11010052
  282.8 21.4 %copy-start.17 = (bf16[1792,1024]{0,1:T(8,128)(2,1)S(1)}, bf16[1792,1024]{0,1:T(8,128)(2,1)}, u32[]{:S(2)}) copy-start(bf16[1792,1024]{0,1:T(8,128)(2,1)} %copy-done.15) | copy-start | bytes 11010052
  288.7 38.6 %collective-permute-start = (bf16[512,1024]{1,0:T(8,128)(2,1)}, bf16[512,1024]{1,0:T(8,128)(2,1)S(1)}, u32[]{:S(2)}, u32[]{:S(2)}) collective-permute-start(bf16[512,1024]{1,0:T(8,128)(2,1)} %fusion.30), channel_id=1, source_target_pairs={{0,4},{4,0},{1,5},{5,1},{2,6},{6,2},{3,7},{7,3},{8,12},{12,8},{9,1... | collective-permute-start | bytes 3145736 | tf_op jit(solution)/shard_map/ppermute | solution.py:24
  307.3 20.6 %collective-permute-start.18 = (bf16[512,1024]{1,0:T(8,128)(2,1)}, bf16[512,1024]{1,0:T(8,128)(2,1)}, u32[]{:S(2)}, u32[]{:S(2)}) collective-permute-start(bf16[512,1024]{1,0:T(8,128)(2,1)} %add_convert_fusion.1), channel_id=1, source_target_pairs={{0,8},{8,16},{16,24},{24,0},{1,9},{9,17},{17,25},{25,1},{2,10},{10... | collective-permute-start | bytes 3145736 | tf_op jit(solution)/shard_map/ppermute | solution.py:20
  (13 other events, 126.2 us)
where the time goes:
time: 331 us
  waiting for transfers between devices  179 us (54%)
  matrix products  64 us (19%)
  other arithmetic  27.8 us (8%)
  starting transfers between devices  27.4 us (8%)
  local copies, waits for them, and re-layouts  24.9 us (8%)
  blocking collectives  6.73 us (2%)
    ppermute x9, waiting for transfers between devices, shift(): lax.ppermute(block, axis, [(i, (i + by) % count) for i in range(count)])  115 us
    ppermute x16, waiting for transfers between devices, swap(): return lax.ppermute(block, axis, [(i, i ^ bit) for i in range(count)])  63.8 us
    dot_general x3, matrix products, shards(): lax.dot_general(grad, act, (((0,), (0,)), ((), ())), preferred_element_ty...  27.1 us
    unnamed x42, local copies, waits for them, and re-layouts  18.4 us
    ppermute x9, starting transfers between devices, shift(): lax.ppermute(block, axis, [(i, (i + by) % count) for i in range(count)])  15 us
    dot_general x4, matrix products, reduced(): jnp.dot(kept, quantized, preferred_element_type=jnp.float32)  14.5 us
    dot_general x4, matrix products, reduced(): jnp.dot(sent, quantized, preferred_element_type=jnp.float32)  14.2 us
    ppermute x16, starting transfers between devices, swap(): return lax.ppermute(block, axis, [(i, i ^ bit) for i in range(count)])  12.3 us
  transfers between devices with their start and end apart: 25, of which 14 were waited for; matrix products, arithmetic and copies ran while one was open for 26% of the time, Pallas kernels for 0%

commit v1 on v0

--- a/solution.py
+++ b/solution.py
@@ -110,7 +110,9 @@
         if running is not None:
             own_total = own_total + running.astype(jnp.float32)
         input_grad = own_total.astype(jnp.bfloat16)
-        step_rows = lax.psum(jnp.sum(products * factor, axis=1) * grad_factor, "col")
+        step_rows = jnp.sum(
+            lax.all_gather(jnp.sum(products * factor, axis=1) * grad_factor, "col"), axis=0
+        )
         weight_grad = (products * inside)[None]
         return (input_grad, weight_grad, step_rows[None])
 

time: 331 us -> 331 us (level)
    psum x1 -> x0, blocking collectives: 6.73 us -> none  [shards(): lax.psum(jnp.sum(products * factor, axis=1) * grad_factor, 'col')]
    all_gather x0 -> x1, blocking collectives: none -> 5.22 us  [shards(): lax.all_gather(jnp.sum(products * factor, axis=1) * grad_factor, 'col')]
    unnamed x42 -> x43, local copies, waits for them, and re-layouts: 18.4 us -> 18.5 us
where the time goes in v1:
time: 331 us
  waiting for transfers between devices  180 us (54%)
  matrix products  64 us (19%)
  other arithmetic  27.8 us (8%)
  starting transfers between devices  27.4 us (8%)
  local copies, waits for them, and re-layouts  25.5 us (8%)
  blocking collectives  5.22 us (2%)
    ppermute x9, waiting for transfers between devices, shift(): lax.ppermute(block, axis, [(i, (i + by) % count) for i in range(count)])  116 us
    ppermute x16, waiting for transfers between devices, swap(): return lax.ppermute(block, axis, [(i, i ^ bit) for i in range(count)])  63.8 us
    dot_general x3, matrix products, shards(): lax.dot_general(grad, act, (((0,), (0,)), ((), ())), preferred_element_ty...  27.1 us
    unnamed x43, local copies, waits for them, and re-layouts  18.5 us
    ppermute x9, starting transfers between devices, shift(): lax.ppermute(block, axis, [(i, (i + by) % count) for i in range(count)])  15 us
    dot_general x4, matrix products, reduced(): jnp.dot(kept, quantized, preferred_element_type=jnp.float32)  14.5 us
    dot_general x4, matrix products, reduced(): jnp.dot(sent, quantized, preferred_element_type=jnp.float32)  14.2 us
    ppermute x16, starting transfers between devices, swap(): return lax.ppermute(block, axis, [(i, i ^ bit) for i in range(count)])  12.3 us
  transfers between devices with their start and end apart: 25, of which 14 were waited for; matrix products, arithmetic and copies ran while one was open for 26% of the time, Pallas kernels for 0%

profile of v1, /device:TPU:0, one launch (start us, length us, event | category | flops | bytes accessed | tf_op | source)
XLA Modules:
  0.0 330.7 jit_solution(12303775881280463528)
XLA Ops:
  6.3 4.7 %fusion.58 = (bf16[256,1792]{1,0:T(8,128)(2,1)}, bf16[256,1792]{1,0:T(8,128)(2,1)}, bf16[256,1792]{1,0:T(8,128)(2,1)S(1)}) fusion(bf16[1024,7168]{1,0:T(8,128)(2,1)} %param.5, s32[]{:T(128)S(6)} %select_n.223, s32[]{:T(128)S(6)} %select_n.226, s32[]{:T(128)S(6)} %select_n.237, s32[]{:T(128)S(6)} %select_n.248), kind=kLoop, calls=%fused_computation.92 | loop fusion | bytes 5505040 | tf_op jit(solution)/shard_map/dynamic_slice | solution.py:64
  12.6 20.0 %collective-permute-done.19 = bf16[512,1024]{1,0:T(8,128)(2,1)S(1)} collective-permute-done((bf16[512,1024]{1,0:T(8,128)(2,1)}, bf16[512,1024]{1,0:T(8,128)(2,1)S(1)}, u32[]{:S(2)}, u32[]{:S(2)}) %collective-permute-start.19) | collective-permute-done | bytes 1048608 | tf_op jit(solution)/shard_map/ppermute | solution.py:20
  36.1 16.3 %collective-permute-done.11 = bf16[256,1792]{1,0:T(8,128)(2,1)} collective-permute-done((bf16[256,1792]{1,0:T(8,128)(2,1)S(1)}, bf16[256,1792]{1,0:T(8,128)(2,1)}, u32[]{:S(2)}, u32[]{:S(2)}) %collective-permute-start.11) | collective-permute-done | bytes 917536 | tf_op jit(solution)/shard_map/ppermute | solution.py:20
  54.1 8.4 %copy.9 = f32[1,1792,1024]{1,2,0:T(8,128)} copy(f32[1,1792,1024]{2,1,0:T(8,128)} %param.6) | data formatting | bytes 14680064 | tf_op args[2]
  63.3 7.9 %collective-permute-done.1 = bf16[256,1792]{1,0:T(8,128)(2,1)} collective-permute-done((bf16[256,1792]{1,0:T(8,128)(2,1)}, bf16[256,1792]{1,0:T(8,128)(2,1)}, u32[]{:S(2)}, u32[]{:S(2)}) %collective-permute-start.1) | collective-permute-done | bytes 917536 | tf_op jit(solution)/shard_map/ppermute | solution.py:20
  72.7 37.7 %collective-permute-done.6 = bf16[256,1792]{1,0:T(8,128)(2,1)} collective-permute-done((bf16[256,1792]{1,0:T(8,128)(2,1)}, bf16[256,1792]{1,0:T(8,128)(2,1)}, u32[]{:S(2)}, u32[]{:S(2)}) %collective-permute-start.6) | collective-permute-done | bytes 917536 | tf_op jit(solution)/shard_map/ppermute | solution.py:20
  112.0 8.2 %fusion.1 = f32[1792,1024]{0,1:T(8,128)} fusion(bf16[1024,1024]{1,0:T(8,128)(2,1)S(1)} %copy-done, bf16[1024,7168]{1,0:T(8,128)(2,1)} %param.5, s32[]{:T(128)S(6)} %select_n.216), kind=kOutput, calls=%fused_computation.12 | convolution fusion | flops 3758096384 | bytes 13107204 | tf_op jit(solution)/shard_map/dot_general | solution.py:95
  122.3 10.7 %collective-permute-done.7 = bf16[256,1792]{1,0:T(8,128)(2,1)S(1)} collective-permute-done((bf16[256,1792]{1,0:T(8,128)(2,1)}, bf16[256,1792]{1,0:T(8,128)(2,1)S(1)}, u32[]{:S(2)}, u32[]{:S(2)}) %collective-permute-start.7) | collective-permute-done | bytes 917536 | tf_op jit(solution)/shard_map/ppermute | solution.py:24
  132.9 5.6 %collective-permute-done.21 = bf16[512,1024]{1,0:T(8,128)(2,1)S(1)} collective-permute-done((bf16[512,1024]{1,0:T(8,128)(2,1)S(1)}, bf16[512,1024]{1,0:T(8,128)(2,1)S(1)}, u32[]{:S(2)}, u32[]{:S(2)}) %collective-permute-start.21) | collective-permute-done | bytes 1048608 | tf_op jit(solution)/shard_map/ppermute | solution.py:20
  141.9 6.7 %fusion.3 = f32[1792,1024]{0,1:T(8,128)} fusion(bf16[512,1024]{1,0:T(8,128)(2,1)S(1)} %get-tuple-element.30, bf16[512,1024]{1,0:T(8,128)(2,1)S(1)} %get-tuple-element.29, bf16[256,1792]{1,0:T(8,128)(2,1)S(1)} %get-tuple-element.26, bf16[256,1792]{1,0:T(8,128)(2,1)S(1)} %get-tuple-element.25, bf16[256,1792]{1,0:T(8,128)(2,1)S(1)} %get-tuple-element.24, ...), kind=kOutput, calls=%fused_computation.14 | convolution fusion | flops 3776970752 | bytes 13107200 | tf_op jit(solution)/shard_map/dot_general | solution.py:107
  148.6 6.0 %collective-permute-start.23 = (bf16[512,1024]{1,0:T(8,128)(2,1)S(1)}, bf16[512,1024]{1,0:T(8,128)(2,1)S(1)}, u32[]{:S(2)}, u32[]{:S(2)}) collective-permute-start(bf16[512,1024]{1,0:T(8,128)(2,1)S(1)} %collective-permute-done.21), channel_id=1, source_target_pairs={{0,8},{8,16},{16,24},{24,0},{1,9},{9,17},{17,25},{25,1},{2,10},{10... | collective-permute-start | bytes 3145736 | tf_op jit(solution)/shard_map/ppermute | solution.py:20
  154.6 3.3 broadcast_select_fusion.29
  159.4 17.6 %collective-permute-done.23 = bf16[512,1024]{1,0:T(8,128)(2,1)S(1)} collective-permute-done((bf16[512,1024]{1,0:T(8,128)(2,1)S(1)}, bf16[512,1024]{1,0:T(8,128)(2,1)S(1)}, u32[]{:S(2)}, u32[]{:S(2)}) %collective-permute-start.23) | collective-permute-done | bytes 1048608 | tf_op jit(solution)/shard_map/ppermute | solution.py:20
  179.7 6.7 %fusion.7 = f32[1792,1024]{0,1:T(8,128)} fusion(bf16[512,1024]{1,0:T(8,128)(2,1)S(1)} %get-tuple-element.32, bf16[512,1024]{1,0:T(8,128)(2,1)S(1)} %get-tuple-element.31, bf16[256,1792]{1,0:T(8,128)(2,1)S(1)} %get-tuple-element.22, bf16[256,1792]{1,0:T(8,128)(2,1)S(1)} %get-tuple-element.21, bf16[256,1792]{1,0:T(8,128)(2,1)S(1)} %get-tuple-element.20, ...), kind=kOutput, calls=%fused_computation.18 | convolution fusion | flops 3776970752 | bytes 13107200 | tf_op jit(solution)/shard_map/dot_general | solution.py:107
  186.4 14.6 %collective-permute-done.24 = bf16[512,1024]{1,0:T(8,128)(2,1)S(1)} collective-permute-done((bf16[512,1024]{1,0:T(8,128)(2,1)S(1)}, bf16[512,1024]{1,0:T(8,128)(2,1)S(1)}, u32[]{:S(2)}, u32[]{:S(2)}) %collective-permute-start.24) | collective-permute-done | bytes 1048608 | tf_op jit(solution)/shard_map/ppermute | solution.py:24
  202.4 13.7 %add_add_fusion = f32[1792,1024]{0,1:T(8,128)} fusion(f32[1792,1024]{0,1:T(8,128)} %fusion.7, f32[1792,1024]{0,1:T(8,128)} %fusion.1, f32[1792,1024]{0,1:T(8,128)} %fusion.3, bf16[512,1024]{1,0:T(8,128)(2,1)} %get-tuple-element.28, bf16[512,1024]{1,0:T(8,128)(2,1)} %get-tuple-element.27, bf16[256,1792]{1,0:T(8,128)(2,1)} %get-tuple-element.18, ...), kind=kOutput, calls=%fused_computation.5 | convolution fusion | flops 3782475776 | bytes 35127296 | tf_op jit(solution)/shard_map/dot_general | solution.py:107
  216.2 8.0 %multiply_reduce_fusion = (f32[1792]{0:T(1024)S(1)}, f32[1,1792,1024]{1,2,0:T(8,128)}, bf16[1792,1024]{0,1:T(8,128)(2,1)S(1)}) fusion(f32[1792,1024]{0,1:T(8,128)} %add_add_fusion, f32[1792]{0:T(1024)S(1)} %dynamic-slice_reduce_fusion, f32[1,1792,1024]{1,2,0:T(8,128)S(1)} %bitcast.20), kind=kLoop, calls=%fused_computation.4 | loop fusion | flops 29358336 | bytes 25704448 | tf_op jit(solution)/shard_map/reduce_sum | solution.py:114
  224.2 3.1 fusion.39
  227.7 5.1 %pad_maximum_fusion.1 = bf16[1024,1792]{1,0:T(8,128)(2,1)S(1)} fusion(bf16[256,1792]{1,0:T(8,128)(2,1)} %copy-done.14, bf16[256,1792]{1,0:T(8,128)(2,1)} %copy-done.13, bf16[256,1792]{1,0:T(8,128)(2,1)S(1)} %copy-done.12, bf16[256,1792]{1,0:T(8,128)(2,1)S(1)} %copy-done.10), kind=kLoop, calls=%fused_computation.10 | loop fusion | flops 14680064 | bytes 7340032 | tf_op jit(solution)/shard_map/concatenate | solution.py:43
  236.6 17.0 %collective-permute-done.15 = bf16[512,1024]{1,0:T(8,128)(2,1)} collective-permute-done((bf16[512,1024]{1,0:T(8,128)(2,1)}, bf16[512,1024]{1,0:T(8,128)(2,1)}, u32[]{:S(2)}, u32[]{:S(2)}) %collective-permute-start.15) | collective-permute-done | bytes 1048608 | tf_op jit(solution)/shard_map/ppermute | solution.py:24
  253.6 3.3 %add_convert_fusion.3 = bf16[512,1024]{1,0:T(8,128)(2,1)S(1)} fusion(bf16[512,1024]{1,0:T(8,128)(2,1)} %collective-permute-done.15, bf16[1792,1024]{0,1:T(8,128)(2,1)S(1)} %copy-done.16, bf16[1024,1792]{1,0:T(8,128)(2,1)S(1)} %copy-done.3, s32[]{:T(128)S(6)} %select_n.214), kind=kOutput, calls=%fused_computation.28 | convolution fusion | flops 1880621056 | bytes 7602180 | tf_op jit(solution)/shard_map/dot_general | solution.py:82
  259.9 3.1 fusion.33
  263.6 12.4 %collective-permute-done.10 = bf16[512,1024]{1,0:T(8,128)(2,1)S(1)} collective-permute-done((bf16[512,1024]{1,0:T(8,128)(2,1)S(1)}, bf16[512,1024]{1,0:T(8,128)(2,1)S(1)}, u32[]{:S(2)}, u32[]{:S(2)}) %collective-permute-start.10) | collective-permute-done | bytes 1048608 | tf_op jit(solution)/shard_map/ppermute | solution.py:24
  275.9 3.7 %collective-permute-done.16 = bf16[512,1024]{1,0:T(8,128)(2,1)S(1)} collective-permute-done((bf16[512,1024]{1,0:T(8,128)(2,1)S(1)}, bf16[512,1024]{1,0:T(8,128)(2,1)S(1)}, u32[]{:S(2)}, u32[]{:S(2)}) %collective-permute-start.16) | collective-permute-done | bytes 1048608 | tf_op jit(solution)/shard_map/ppermute | solution.py:20
  279.7 3.1 add_convert_fusion.2
  282.8 5.9 %fusion.30 = bf16[512,1024]{1,0:T(8,128)(2,1)} fusion(bf16[1792,1024]{0,1:T(8,128)(2,1)} %copy-done.15, bf16[1024,7168]{1,0:T(8,128)(2,1)} %param.5, s32[]{:T(128)S(6)} %select_n.219, s32[]{:T(128)S(6)} %select_n.217), kind=kOutput, calls=%fused_computation.45 | convolution fusion | flops 1879572480 | bytes 6553608 | tf_op jit(solution)/shard_map/dot_general | solution.py:80
  289.2 9.2 %collective-permute-done.5 = bf16[512,1024]{1,0:T(8,128)(2,1)S(1)} collective-permute-done((bf16[512,1024]{1,0:T(8,128)(2,1)}, bf16[512,1024]{1,0:T(8,128)(2,1)S(1)}, u32[]{:S(2)}, u32[]{:S(2)}) %collective-permute-start.5) | collective-permute-done | bytes 1048608 | tf_op jit(solution)/shard_map/ppermute | solution.py:24
  298.4 5.7 %collective-permute-done.17 = bf16[512,1024]{1,0:T(8,128)(2,1)S(1)} collective-permute-done((bf16[512,1024]{1,0:T(8,128)(2,1)}, bf16[512,1024]{1,0:T(8,128)(2,1)S(1)}, u32[]{:S(2)}, u32[]{:S(2)}) %collective-permute-start.17) | collective-permute-done | bytes 1048608 | tf_op jit(solution)/shard_map/ppermute | solution.py:20
  304.2 3.1 add_convert_fusion.1
  307.3 8.4 %copy.10 = f32[1,1792,1024]{2,1,0:T(8,128)} copy(f32[1,1792,1024]{1,2,0:T(8,128)} %get-tuple-element.10) | data formatting | bytes 14680064
  315.7 5.2 %all-gather.1 = f32[4,1,1792]{2,1,0:T(1,128)S(1)} all-gather(f32[1,1,1792]{2,1,0:T(1,128)S(1)} %reshape.19), channel_id=2, replica_groups=mesh['dp'=4,'row'=2,'col'=4] {'col'}, dimensions={0}, use_global_device_ids=true | all-gather | bytes 35840 | tf_op jit(solution)/shard_map/all_gather | solution.py:114
  321.5 4.9 %fusion.28 = f32[512,1024]{1,0:T(8,128)S(1)} fusion(bf16[1792,1024]{0,1:T(8,128)(2,1)} %copy-done.15, bf16[1024,7168]{1,0:T(8,128)(2,1)} %param.5, s32[]{:T(128)S(6)} %select_n.215, s32[]{:T(128)S(6)} %select_n.217), kind=kOutput, calls=%fused_computation.43 | convolution fusion | flops 1879048192 | bytes 7602184 | tf_op jit(solution)/shard_map/dot_general | solution.py:82
  (92 shorter events, 40.5 us)
Async XLA Ops:
  3.3 29.3 %collective-permute-start.19 = (bf16[512,1024]{1,0:T(8,128)(2,1)}, bf16[512,1024]{1,0:T(8,128)(2,1)S(1)}, u32[]{:S(2)}, u32[]{:S(2)}) collective-permute-start(bf16[512,1024]{1,0:T(8,128)(2,1)} %constant_dynamic-slice_fusion), channel_id=1, source_target_pairs={{0,8},{8,16},{16,24},{24,0},{1,9},{9,17},{17,25},{25,1},{2,10},{10... | collective-permute-start | bytes 3145736 | tf_op jit(solution)/shard_map/ppermute | solution.py:20
  11.0 41.4 %collective-permute-start.11 = (bf16[256,1792]{1,0:T(8,128)(2,1)S(1)}, bf16[256,1792]{1,0:T(8,128)(2,1)}, u32[]{:S(2)}, u32[]{:S(2)}) collective-permute-start(bf16[256,1792]{1,0:T(8,128)(2,1)S(1)} %get-tuple-element.13), channel_id=1, source_target_pairs={{0,8},{8,16},{16,24},{24,0},{1,9},{9,17},{17,25},{25,1},{2,10},{10... | collective-permute-start | bytes 2752520 | tf_op jit(solution)/shard_map/ppermute | solution.py:20
  32.6 79.4 %collective-permute-start.20 = (bf16[512,1024]{1,0:T(8,128)(2,1)S(1)}, bf16[512,1024]{1,0:T(8,128)(2,1)}, u32[]{:S(2)}, u32[]{:S(2)}) collective-permute-start(bf16[512,1024]{1,0:T(8,128)(2,1)S(1)} %collective-permute-done.19), channel_id=1, source_target_pairs={{0,4},{4,0},{1,5},{5,1},{2,6},{6,2},{3,7},{7,3},{8,12},{12,8},{9,1... | collective-permute-start | bytes 3145736 | tf_op jit(solution)/shard_map/ppermute | solution.py:24
  34.3 36.9 %collective-permute-start.1 = (bf16[256,1792]{1,0:T(8,128)(2,1)}, bf16[256,1792]{1,0:T(8,128)(2,1)}, u32[]{:S(2)}, u32[]{:S(2)}) collective-permute-start(bf16[256,1792]{1,0:T(8,128)(2,1)} %get-tuple-element.11), channel_id=1, source_target_pairs={{0,24},{8,0},{16,8},{24,16},{1,25},{9,1},{17,9},{25,17},{2,26},{10... | collective-permute-start | bytes 2752520 | tf_op jit(solution)/shard_map/ppermute | solution.py:20
  36.1 74.4 %collective-permute-start.6 = (bf16[256,1792]{1,0:T(8,128)(2,1)}, bf16[256,1792]{1,0:T(8,128)(2,1)}, u32[]{:S(2)}, u32[]{:S(2)}) collective-permute-start(bf16[256,1792]{1,0:T(8,128)(2,1)} %get-tuple-element.12), channel_id=1, source_target_pairs={{0,16},{8,24},{16,0},{24,8},{1,17},{9,25},{17,1},{25,9},{2,18},{10... | collective-permute-start | bytes 2752520 | tf_op jit(solution)/shard_map/ppermute | solution.py:20
  52.4 59.6 %collective-permute-start.12 = (bf16[256,1792]{1,0:T(8,128)(2,1)}, bf16[256,1792]{1,0:T(8,128)(2,1)}, u32[]{:S(2)}, u32[]{:S(2)}) collective-permute-start(bf16[256,1792]{1,0:T(8,128)(2,1)} %collective-permute-done.11), channel_id=1, source_target_pairs={{0,2},{1,3},{2,0},{3,1},{4,6},{5,7},{6,4},{7,5},{8,10},{9,11},{10,... | collective-permute-start | bytes 2752520 | tf_op jit(solution)/shard_map/ppermute | solution.py:24
  63.3 58.9 %collective-permute-start.14 = (bf16[256,1792]{1,0:T(8,128)(2,1)}, bf16[256,1792]{1,0:T(8,128)(2,1)S(1)}, u32[]{:S(2)}, u32[]{:S(2)}) collective-permute-start(bf16[256,1792]{1,0:T(8,128)(2,1)} %collective-permute-done.11), channel_id=1, source_target_pairs={{0,1},{1,0},{2,3},{3,2},{4,5},{5,4},{6,7},{7,6},{8,9},{9,8},{10,11... | collective-permute-start | bytes 2752520 | tf_op jit(solution)/shard_map/ppermute | solution.py:24
  71.2 50.4 %collective-permute-start.2 = (bf16[256,1792]{1,0:T(8,128)(2,1)}, bf16[256,1792]{1,0:T(8,128)(2,1)S(1)}, u32[]{:S(2)}, u32[]{:S(2)}) collective-permute-start(bf16[256,1792]{1,0:T(8,128)(2,1)} %collective-permute-done.1), channel_id=1, source_target_pairs={{0,2},{1,3},{2,0},{3,1},{4,6},{5,7},{6,4},{7,5},{8,10},{9,11},{10,... | collective-permute-start | bytes 2752520 | tf_op jit(solution)/shard_map/ppermute | solution.py:24
  110.5 22.4 %collective-permute-start.7 = (bf16[256,1792]{1,0:T(8,128)(2,1)}, bf16[256,1792]{1,0:T(8,128)(2,1)S(1)}, u32[]{:S(2)}, u32[]{:S(2)}) collective-permute-start(bf16[256,1792]{1,0:T(8,128)(2,1)} %collective-permute-done.6), channel_id=1, source_target_pairs={{0,2},{1,3},{2,0},{3,1},{4,6},{5,7},{6,4},{7,5},{8,10},{9,11},{10,... | collective-permute-start | bytes 2752520 | tf_op jit(solution)/shard_map/ppermute | solution.py:24
  112.0 26.6 %collective-permute-start.21 = (bf16[512,1024]{1,0:T(8,128)(2,1)S(1)}, bf16[512,1024]{1,0:T(8,128)(2,1)S(1)}, u32[]{:S(2)}, u32[]{:S(2)}) collective-permute-start(bf16[512,1024]{1,0:T(8,128)(2,1)S(1)} %collective-permute-done.19), channel_id=1, source_target_pairs={{0,8},{8,16},{16,24},{24,0},{1,9},{9,17},{17,25},{25,1},{2,10},{10... | collective-permute-start | bytes 3145736 | tf_op jit(solution)/shard_map/ppermute | solution.py:20
  112.0 26.6 %collective-permute-start.13 = (bf16[256,1792]{1,0:T(8,128)(2,1)}, bf16[256,1792]{1,0:T(8,128)(2,1)S(1)}, u32[]{:S(2)}, u32[]{:S(2)}) collective-permute-start(bf16[256,1792]{1,0:T(8,128)(2,1)} %collective-permute-done.12), channel_id=1, source_target_pairs={{0,1},{1,0},{2,3},{3,2},{4,5},{5,4},{6,7},{7,6},{8,9},{9,8},{10,11... | collective-permute-start | bytes 2752520 | tf_op jit(solution)/shard_map/ppermute | solution.py:24
  121.6 27.0 %collective-permute-start.4 = (bf16[256,1792]{1,0:T(8,128)(2,1)}, bf16[256,1792]{1,0:T(8,128)(2,1)S(1)}, u32[]{:S(2)}, u32[]{:S(2)}) collective-permute-start(bf16[256,1792]{1,0:T(8,128)(2,1)} %collective-permute-done.1), channel_id=1, source_target_pairs={{0,1},{1,0},{2,3},{3,2},{4,5},{5,4},{6,7},{7,6},{8,9},{9,8},{10,11... | collective-permute-start | bytes 2752520 | tf_op jit(solution)/shard_map/ppermute | solution.py:24
  122.2 35.7 %collective-permute-start.9 = (bf16[256,1792]{1,0:T(8,128)(2,1)}, bf16[256,1792]{1,0:T(8,128)(2,1)S(1)}, u32[]{:S(2)}, u32[]{:S(2)}) collective-permute-start(bf16[256,1792]{1,0:T(8,128)(2,1)} %collective-permute-done.6), channel_id=1, source_target_pairs={{0,1},{1,0},{2,3},{3,2},{4,5},{5,4},{6,7},{7,6},{8,9},{9,8},{10,11... | collective-permute-start | bytes 2752520 | tf_op jit(solution)/shard_map/ppermute | solution.py:24
  132.9 21.7 %collective-permute-start.3 = (bf16[256,1792]{1,0:T(8,128)(2,1)S(1)}, bf16[256,1792]{1,0:T(8,128)(2,1)S(1)}, u32[]{:S(2)}, u32[]{:S(2)}) collective-permute-start(bf16[256,1792]{1,0:T(8,128)(2,1)S(1)} %collective-permute-done.2), channel_id=1, source_target_pairs={{0,1},{1,0},{2,3},{3,2},{4,5},{5,4},{6,7},{7,6},{8,9},{9,8},{10,11... | collective-permute-start | bytes 2752520 | tf_op jit(solution)/shard_map/ppermute | solution.py:24
  138.5 19.4 %collective-permute-start.8 = (bf16[256,1792]{1,0:T(8,128)(2,1)S(1)}, bf16[256,1792]{1,0:T(8,128)(2,1)S(1)}, u32[]{:S(2)}, u32[]{:S(2)}) collective-permute-start(bf16[256,1792]{1,0:T(8,128)(2,1)S(1)} %collective-permute-done.7), channel_id=1, source_target_pairs={{0,1},{1,0},{2,3},{3,2},{4,5},{5,4},{6,7},{7,6},{8,9},{9,8},{10,11... | collective-permute-start | bytes 2752520 | tf_op jit(solution)/shard_map/ppermute | solution.py:24
  138.5 41.0 %collective-permute-start.22 = (bf16[512,1024]{1,0:T(8,128)(2,1)S(1)}, bf16[512,1024]{1,0:T(8,128)(2,1)S(1)}, u32[]{:S(2)}, u32[]{:S(2)}) collective-permute-start(bf16[512,1024]{1,0:T(8,128)(2,1)S(1)} %collective-permute-done.21), channel_id=1, source_target_pairs={{0,4},{4,0},{1,5},{5,1},{2,6},{6,2},{3,7},{7,3},{8,12},{12,8},{9,1... | collective-permute-start | bytes 3145736 | tf_op jit(solution)/shard_map/ppermute | solution.py:24
  148.6 28.3 %collective-permute-start.23 = (bf16[512,1024]{1,0:T(8,128)(2,1)S(1)}, bf16[512,1024]{1,0:T(8,128)(2,1)S(1)}, u32[]{:S(2)}, u32[]{:S(2)}) collective-permute-start(bf16[512,1024]{1,0:T(8,128)(2,1)S(1)} %collective-permute-done.21), channel_id=1, source_target_pairs={{0,8},{8,16},{16,24},{24,0},{1,9},{9,17},{17,25},{25,1},{2,10},{10... | collective-permute-start | bytes 3145736 | tf_op jit(solution)/shard_map/ppermute | solution.py:20
  159.4 20.3 %copy-start.9 = (bf16[256,1792]{1,0:T(8,128)(2,1)}, bf16[256,1792]{1,0:T(8,128)(2,1)S(1)}, u32[]{:S(2)}) copy-start(bf16[256,1792]{1,0:T(8,128)(2,1)S(1)} %get-tuple-element.19) | copy-start | bytes 2752516
  177.0 24.0 %collective-permute-start.24 = (bf16[512,1024]{1,0:T(8,128)(2,1)S(1)}, bf16[512,1024]{1,0:T(8,128)(2,1)S(1)}, u32[]{:S(2)}, u32[]{:S(2)}) collective-permute-start(bf16[512,1024]{1,0:T(8,128)(2,1)S(1)} %collective-permute-done.23), channel_id=1, source_target_pairs={{0,4},{4,0},{1,5},{5,1},{2,6},{6,2},{3,7},{7,3},{8,12},{12,8},{9,1... | collective-permute-start | bytes 3145736 | tf_op jit(solution)/shard_map/ppermute | solution.py:24
  227.2 26.4 %collective-permute-start.15 = (bf16[512,1024]{1,0:T(8,128)(2,1)}, bf16[512,1024]{1,0:T(8,128)(2,1)}, u32[]{:S(2)}, u32[]{:S(2)}) collective-permute-start(bf16[512,1024]{1,0:T(8,128)(2,1)} %fusion.39), channel_id=1, source_target_pairs={{0,4},{4,0},{1,5},{5,1},{2,6},{6,2},{3,7},{7,3},{8,12},{12,8},{9,1... | collective-permute-start | bytes 3145736 | tf_op jit(solution)/shard_map/ppermute | solution.py:24
  232.9 20.7 %copy-start.3 = (bf16[1024,1792]{1,0:T(8,128)(2,1)S(1)}, bf16[1024,1792]{1,0:T(8,128)(2,1)}, u32[]{:S(2)}) copy-start(bf16[1024,1792]{1,0:T(8,128)(2,1)} %pad_maximum_fusion.2) | copy-start | bytes 11010052
  235.0 24.6 %copy-start.6 = (bf16[256,1792]{1,0:T(8,128)(2,1)S(1)}, bf16[256,1792]{1,0:T(8,128)(2,1)}, u32[]{:S(2)}) copy-start(bf16[256,1792]{1,0:T(8,128)(2,1)} %get-tuple-element.16) | copy-start | bytes 2752516
  235.0 24.5 %copy-start.7 = (bf16[256,1792]{1,0:T(8,128)(2,1)S(1)}, bf16[256,1792]{1,0:T(8,128)(2,1)}, u32[]{:S(2)}) copy-start(bf16[256,1792]{1,0:T(8,128)(2,1)} %get-tuple-element.17) | copy-start | bytes 2752516
  235.0 24.5 %copy-start.8 = (bf16[256,1792]{1,0:T(8,128)(2,1)S(1)}, bf16[256,1792]{1,0:T(8,128)(2,1)}, u32[]{:S(2)}) copy-start(bf16[256,1792]{1,0:T(8,128)(2,1)} %get-tuple-element.18) | copy-start | bytes 2752516
  235.0 40.9 %collective-permute-start.10 = (bf16[512,1024]{1,0:T(8,128)(2,1)S(1)}, bf16[512,1024]{1,0:T(8,128)(2,1)S(1)}, u32[]{:S(2)}, u32[]{:S(2)}) collective-permute-start(bf16[512,1024]{1,0:T(8,128)(2,1)S(1)} %fusion.36), channel_id=1, source_target_pairs={{0,4},{4,0},{1,5},{5,1},{2,6},{6,2},{3,7},{7,3},{8,12},{12,8},{9,1... | collective-permute-start | bytes 3145736 | tf_op jit(solution)/shard_map/ppermute | solution.py:24
  256.9 22.8 %collective-permute-start.16 = (bf16[512,1024]{1,0:T(8,128)(2,1)S(1)}, bf16[512,1024]{1,0:T(8,128)(2,1)S(1)}, u32[]{:S(2)}, u32[]{:S(2)}) collective-permute-start(bf16[512,1024]{1,0:T(8,128)(2,1)S(1)} %add_convert_fusion.3), channel_id=1, source_target_pairs={{0,8},{8,16},{16,24},{24,0},{1,9},{9,17},{17,25},{25,1},{2,10},{10... | collective-permute-start | bytes 3145736 | tf_op jit(solution)/shard_map/ppermute | solution.py:20
  263.1 35.4 %collective-permute-start.5 = (bf16[512,1024]{1,0:T(8,128)(2,1)}, bf16[512,1024]{1,0:T(8,128)(2,1)S(1)}, u32[]{:S(2)}, u32[]{:S(2)}) collective-permute-start(bf16[512,1024]{1,0:T(8,128)(2,1)} %fusion.33), channel_id=1, source_target_pairs={{0,4},{4,0},{1,5},{5,1},{2,6},{6,2},{3,7},{7,3},{8,12},{12,8},{9,1... | collective-permute-start | bytes 3145736 | tf_op jit(solution)/shard_map/ppermute | solution.py:24
  282.8 21.4 %collective-permute-start.17 = (bf16[512,1024]{1,0:T(8,128)(2,1)}, bf16[512,1024]{1,0:T(8,128)(2,1)S(1)}, u32[]{:S(2)}, u32[]{:S(2)}) collective-permute-start(bf16[512,1024]{1,0:T(8,128)(2,1)} %add_convert_fusion.2), channel_id=1, source_target_pairs={{0,8},{8,16},{16,24},{24,0},{1,9},{9,17},{17,25},{25,1},{2,10},{10... | collective-permute-start | bytes 3145736 | tf_op jit(solution)/shard_map/ppermute | solution.py:20
  282.8 21.4 %copy-start.5 = (bf16[1024,1792]{1,0:T(8,128)(2,1)S(1)}, bf16[1024,1792]{1,0:T(8,128)(2,1)}, u32[]{:S(2)}) copy-start(bf16[1024,1792]{1,0:T(8,128)(2,1)} %copy-done.4) | copy-start | bytes 11010052
  282.8 21.4 %copy-start.17 = (bf16[1792,1024]{0,1:T(8,128)(2,1)S(1)}, bf16[1792,1024]{0,1:T(8,128)(2,1)}, u32[]{:S(2)}) copy-start(bf16[1792,1024]{0,1:T(8,128)(2,1)} %copy-done.15) | copy-start | bytes 11010052
  288.7 37.8 %collective-permute-start = (bf16[512,1024]{1,0:T(8,128)(2,1)}, bf16[512,1024]{1,0:T(8,128)(2,1)S(1)}, u32[]{:S(2)}, u32[]{:S(2)}) collective-permute-start(bf16[512,1024]{1,0:T(8,128)(2,1)} %fusion.30), channel_id=1, source_target_pairs={{0,4},{4,0},{1,5},{5,1},{2,6},{6,2},{3,7},{7,3},{8,12},{12,8},{9,1... | collective-permute-start | bytes 3145736 | tf_op jit(solution)/shard_map/ppermute | solution.py:24
  307.3 20.6 %collective-permute-start.18 = (bf16[512,1024]{1,0:T(8,128)(2,1)}, bf16[512,1024]{1,0:T(8,128)(2,1)}, u32[]{:S(2)}, u32[]{:S(2)}) collective-permute-start(bf16[512,1024]{1,0:T(8,128)(2,1)} %add_convert_fusion.1), channel_id=1, source_target_pairs={{0,8},{8,16},{16,24},{24,0},{1,9},{9,17},{17,25},{25,1},{2,10},{10... | collective-permute-start | bytes 3145736 | tf_op jit(solution)/shard_map/ppermute | solution.py:20
  (13 other events, 127.1 us)
